TPU v7x, 32 devices: a whole 2x2x4 slice. The times are simulated.
32 devices in a mesh: freq: 4 (over y, core), mesh: 8 (over z, x).
Axes of the slice: x: 2, y: 2, z: 4, core: 2. Of those that a mesh axis runs over, the one named last changes fastest.
Arguments:
- spectrum: float32 [2, 216, 32768], P(None, 'freq', 'mesh'), may hold values from -84 to 84
- time_weights: float32 [2, 432], P(None, 'freq'), may hold values from -0.625 to 0.625
- interp_weights: float32 [1024, 128, 128], P('mesh'), may hold values from -0.5 to 0.5
- group_block: int32 [1024], P('mesh'), may hold values from 0 to 255, as said below
- group_count: int32 [8], P('mesh'), may hold values from 64 to 128, as said below
- wave_state: float32 [4, 2, 524288], P('freq', None, 'mesh'), may hold values from -6 to 6
- neighbors: int32 [4, 4096], P(None, 'mesh'), may hold values from 0 to 575, as said below
- coupling: float32 [4, 524288], P(None, 'mesh'), may hold values from 0.02 to 0.2
Outputs:
- series: float32 [432, 32768], P('freq', 'mesh')
- new_state: float32 [4, 2, 524288], P('freq', None, 'mesh')
Inputs may be any that keep to these rules, and one draw needn't show every extreme that they name: `group_block`: partition o owns blocks o * 32 to o * 32 + 31. Of one partition's 128 groups at most 16 name blocks of one owner, and each partition has an owner named by exactly 16 of its live groups. The live groups of partition m are its first group_count[m]; some partition has exactly 128. `neighbors`: for the cell row with local row index u, a value e names local row e - 32 of the row's own partition when it lies in 32 .. (69632) // 128 - 1, else a row of the neighbouring partition below or above; never the row itself.
All inputs are finite; a program needn't handle non-finite values.
Results may differ from a plain program's by a relative error of at most 0.0001.
Values sent between devices are 32-bit elements; how exact they have to be, the bound alone decides.
No kernel may reach another device: no remote copies, remote signals or barrier semaphores. Data moves between devices by JAX's collectives and lax.ppermute only.
A program may use at most 64 MiB of HBM per device.

v0:
```python
import math

import jax
import jax.numpy as jnp
from jax import lax
from jax.experimental import pallas as pl
from jax.experimental.pallas import tpu as pltpu
from jax.sharding import PartitionSpec as P


HB = 4096

high = lax.Precision.HIGH


def basis(times, first, count, horizon):
    column = lax.iota(jnp.int32, 2 * count)
    freqs = first + column // 2
    phase = (times[:, None] * freqs[None, :] % horizon).astype(jnp.float32)
    angles = phase * (2.0 * math.pi / horizon)
    scales = jnp.where(freqs == 0, 1.0, 2.0).astype(jnp.float32) / horizon
    return jnp.where(column % 2 == 0, jnp.cos(angles), -jnp.sin(angles)) * scales


def mm(a, b):
    return jnp.dot(a, b, precision=high, preferred_element_type=jnp.float32)


def spread_rows(nbr_ref, coup_ref, ext_ref, got_ref, rows):
    faces = coup_ref.shape[0]
    unroll = 8

    def body(i, carry):
        for j in range(unroll):
            u = i * unroll + j
            for n in range(faces):
                got_ref[n, pl.ds(u, 1), :] = ext_ref[pl.ds(nbr_ref[n, u], 1), :]
        return carry

    lax.fori_loop(0, rows // unroll, body, 0)


def first_kernel(nbr_ref, low_ref, high_ref, state_ref, coup_ref, out_ref, ext_ref, got_ref):
    rows = state_ref.shape[1]
    halo = low_ref.shape[0]
    ext_ref[pl.ds(0, halo), :] = low_ref[...]
    ext_ref[pl.ds(halo, rows), :] = state_ref[1]
    ext_ref[pl.ds(halo + rows, halo), :] = high_ref[...]
    spread_rows(nbr_ref, coup_ref, ext_ref, got_ref, rows)
    cur = state_ref[1]
    total = 2.0 * cur - state_ref[0]
    for n in range(coup_ref.shape[0]):
        total = total + coup_ref[n] * (got_ref[n] - cur)
    out_ref[...] = total


def second_kernel(
    nbr_ref, low_ref, high_ref, base_ref, prev_ref, push_ref, coup_ref, out_ref, ext_ref, got_ref
):
    rows = base_ref.shape[0]
    halo = low_ref.shape[0]
    groups = push_ref.shape[1]
    ext_ref[pl.ds(0, halo), :] = low_ref[...]
    ext_ref[pl.ds(halo, rows), :] = base_ref[...]
    ext_ref[pl.ds(halo, groups), :] = base_ref[pl.ds(0, groups), :] + push_ref[0]
    ext_ref[pl.ds(halo + rows, halo), :] = high_ref[...]
    spread_rows(nbr_ref, coup_ref, ext_ref, got_ref, rows)
    cur = ext_ref[pl.ds(halo, rows), :]
    out_ref[0] = cur
    total = 2.0 * cur - prev_ref[...]
    for n in range(coup_ref.shape[0]):
        total = total + coup_ref[n] * (got_ref[n] - cur)
    out_ref[1] = total
    out_ref[1, pl.ds(0, groups), :] = out_ref[1, pl.ds(0, groups), :] + push_ref[1]


def call(kernel, out_shape, rows, lanes, halo, faces, args):
    vmem = pl.BlockSpec(memory_space=pltpu.VMEM)
    smem = pl.BlockSpec(memory_space=pltpu.SMEM)
    return pl.pallas_call(
        kernel,
        out_shape=jax.ShapeDtypeStruct(out_shape, jnp.float32),
        in_specs=[smem] + [vmem] * (len(args) - 1),
        out_specs=vmem,
        scratch_shapes=[
            pltpu.VMEM((rows + 2 * halo, lanes), jnp.float32),
            pltpu.VMEM((faces, rows, lanes), jnp.float32),
        ],
    )(*args)


def body(
    spectrum,
    time_weights,
    interp_weights,
    group_block,
    group_count,
    wave_state,
    neighbors,
    coupling,
):
    parts, local_freqs, points = spectrum.shape
    nf = lax.axis_size("freq")
    nm = lax.axis_size("mesh")
    me = lax.axis_index("freq")
    horizon = 2 * local_freqs * nf
    window = horizon // nf
    cores = 2 if nf % 2 == 0 else 1
    chips = nf // cores

    def across(x, d):
        return lax.ppermute(x, "freq", [(i, (i + d * cores) % nf) for i in range(nf)])

    def beside(x):
        return lax.ppermute(x, "freq", [(i, i ^ 1) for i in range(nf)])

    width = parts * local_freqs
    stacked = jnp.transpose(spectrum, (1, 0, 2)).reshape(width, points)
    step = max(8, -(-3 * width // 8) // 8 * 8)
    cuts = [(at, min(at + step, width)) for at in range(0, width, step)]

    groups, block = interp_weights.shape[:2]
    faces, rows = neighbors.shape
    lanes = wave_state.shape[2] // rows
    halo = HB // lanes
    up = [(i, i + 1) for i in range(nm - 1)]
    down = [(i + 1, i) for i in range(nm - 1)]
    state = wave_state.reshape(2, rows, lanes)
    coup = coupling.reshape(faces, rows, lanes)
    low0 = lax.ppermute(state[1, rows - halo :], "mesh", up)
    high0 = lax.ppermute(state[1, :halo], "mesh", down)

    weights = lax.all_gather(time_weights, "freq", axis=0)
    times = lax.iota(jnp.int32, horizon)
    basis_own = basis(times, me * local_freqs, local_freqs, horizon).reshape(nf, window, width)
    folded = jnp.einsum(
        "wsr,wrk->wsk", weights, basis_own, precision=lax.Precision.HIGHEST
    ).reshape(nf * 2, width)
    weights, stacked = lax.optimization_barrier((weights, stacked))
    mate = beside(stacked) if cores == 2 else None
    head = [across(stacked[slice(*cuts[0])], d) for d in range(1, chips)]
    partial = mm(folded, stacked)
    per_owner = points // block
    partial = partial.reshape(nf, 2 * per_owner, block)
    weighted = jnp.sum(
        lax.all_to_all(partial, "freq", split_axis=0, concat_axis=0, tiled=True), axis=0
    )
    table = lax.all_gather(weighted, "mesh", axis=0, tiled=True)
    table, stacked_late = lax.optimization_barrier((table, stacked))
    tails = [
        [across(stacked_late[slice(*cut)], d) for d in range(1, chips)] for cut in cuts[1:]
    ]

    base = call(
        first_kernel, (rows, lanes), rows, lanes, halo, faces,
        (neighbors, low0, high0, state, coup),
    )

    owner = group_block // per_owner
    index = owner * (2 * per_owner) + group_block % per_owner
    live = (lax.iota(jnp.int32, groups) < group_count[0]).astype(jnp.float32)
    index = jnp.concatenate([index, index + per_owner])
    picked = table.at[index].get(mode="promise_in_bounds").reshape(2, groups, block)
    picked = picked * live[None, :, None]
    push = jnp.einsum("rgp,gfp->rgf", picked, interp_weights, precision=high)

    edge = base[:halo] + push[0, :halo]
    high1 = lax.ppermute(edge, "mesh", down)
    low1 = lax.ppermute(base[rows - halo :], "mesh", up)
    new_state = call(
        second_kernel, (2, rows, lanes), rows, lanes, halo, faces,
        (neighbors, low1, high1, base, state[1], push, coup),
    )
    if tails:
        new_state, tails[-1] = lax.optimization_barrier((new_state, tails[-1]))
    new_state = new_state.reshape(1, 2, rows * lanes)

    my_times = me * window + lax.iota(jnp.int32, window)

    def table_of(source):
        return basis(my_times, source * local_freqs, local_freqs, horizon)

    series = mm(table_of(me), stacked)
    if cores == 2:
        series = series + mm(table_of(me ^ 1), mate)
    far = [(me - d * cores) % nf for d in range(1, chips)]
    far_tables = [(table_of(f), table_of(f ^ 1)) for f in far]
    for cut, arrived in zip(cuts, [head] + tails):
        for (here, there), x in zip(far_tables, arrived):
            if cores == 2:
                passed = beside(x)
                series = series + mm(here[:, slice(*cut)], x)
                series = series + mm(there[:, slice(*cut)], passed)
            else:
                series = series + mm(here[:, slice(*cut)], x)
    return (series, new_state)


def solution(mesh):
    placed = (
        P(None, "freq", "mesh"),
        P(None, "freq"),
        P("mesh", None, None),
        P("mesh"),
        P("mesh"),
        P("freq", None, "mesh"),
        P(None, "mesh"),
        P(None, "mesh"),
    )
    return jax.shard_map(
        body,
        mesh=mesh,
        in_specs=placed,
        out_specs=(P("freq", "mesh"), P("freq", None, "mesh")),
        check_vma=False,
    )
```

profile of v0, /device:TPU:0, one launch (start us, length us, event | category | flops | bytes accessed | tf_op | source)
XLA Modules:
  0.0 114.4 jit_solution(346442362760718486)
XLA Ops:
  0.6 6.3 %all-gather.1 = f32[4,2,108]{2,1,0:T(2,128)S(1)} all-gather(f32[1,2,108]{2,1,0:T(2,128)} %bitcast.58), channel_id=2, replica_groups=mesh['freq'=4,'mesh'=8] {'freq'}, dimensions={0}, use_global_device_ids=true | all-gather | bytes 4320 | tf_op jit(solution)/shard_map/all_gather | solution.py:133
  6.9 2.5 %reshape.186 = f32[108,4096]{1,0:T(8,128)S(1)} reshape(f32[54,2,4096]{2,1,0:T(2,128)} %bitcast.49) | data formatting | bytes 3538944 | tf_op jit(solution)/shard_map/reshape | solution.py:118
  9.5 0.4 collective-permute-start
  9.9 0.9 slice.47
  10.8 2.0 %collective-permute-start.1 = (f32[40,4096]{1,0:T(8,128)}, f32[40,4096]{1,0:T(8,128)}, u32[]{:S(2)}, u32[]{:S(2)}) collective-permute-start(f32[40,4096]{1,0:T(8,128)} %slice.47), channel_id=1, source_target_pairs={{0,16},{8,24},{16,0},{24,8},{1,17},{9,25},{17,1},{25,9},{2,18},{10... | collective-permute-start | bytes 1966088 | tf_op jit(solution)/shard_map/ppermute | solution.py:112
  12.8 1.6 %fusion.5 = f32[4,108,2]{1,2,0:T(2,128)S(1)} fusion(f32[4,2,108]{2,1,0:T(2,128)S(1)} %all-gather.1, f32[108]{0:T(128)S(1)} %fusion.86, s32[108]{0:T(128)S(1)} %broadcast_add_fusion.3, s32[4,108]{1,0:T(4,128)S(1)} %multiply_add_fusion, pred[108]{0:T(512)(128)(4,1)S(1)} %fusion.85), kind=kOutput, calls=%fused_computation.13 | convolution fusion | flops 1679616 | bytes 9612 | tf_op jit(solution)/shard_map/wsr,wrk->wsk/dot_general | solution.py:136
  14.3 0.6 fusion.100
  14.9 0.7 reshape.188
  15.6 3.3 %all-to-all-start = ((f32[4,64,128]{2,1,0:T(8,128)}), f32[4,64,128]{2,1,0:T(8,128)S(1)}, u32[]{:S(2)}, u32[]{:S(2)}) async-start(f32[4,64,128]{2,1,0:T(8,128)} %reshape.188), calls=%async_computation | async-start | bytes 262144 | tf_op jit(solution)/shard_map/all_to_all | solution.py:146
  18.9 0.0 copy-done.2
  19.0 0.0 copy-start.1
  19.0 3.4 %collective-permute-start.5 = (f32[32,128]{1,0:T(8,128)S(1)}, f32[32,128]{1,0:T(8,128)S(1)}, u32[]{:S(2)}, u32[]{:S(2)}) collective-permute-start(f32[32,128]{1,0:T(8,128)S(1)} %get-tuple-element.15), channel_id=1, source_target_pairs={{0,1},{1,2},{2,3},{3,4},{4,5},{5,6},{6,7},{8,9},{9,10},{10,11},{11... | collective-permute-start | bytes 49160 | tf_op jit(solution)/shard_map/ppermute | solution.py:130
  22.4 1.3 %collective-permute-start.6 = (f32[32,128]{1,0:T(8,128)S(1)}, f32[32,128]{1,0:T(8,128)S(1)}, u32[]{:S(2)}, u32[]{:S(2)}) collective-permute-start(f32[32,128]{1,0:T(8,128)S(1)} %get-tuple-element.14), channel_id=1, source_target_pairs={{1,0},{2,1},{3,2},{4,3},{5,4},{6,5},{7,6},{9,8},{10,9},{11,10},{12... | collective-permute-start | bytes 49160 | tf_op jit(solution)/shard_map/ppermute | solution.py:131
  23.7 0.6 fusion.88
  24.3 0.6 broadcast_add_fusion
  24.9 2.4 %fusion.54 = f32[108,4096]{1,0:T(8,128)} fusion(f32[108,4096]{1,0:T(8,128)S(1)} %reshape.186, f32[108]{0:T(128)S(1)} %fusion.86, s32[108]{0:T(128)S(1)} %broadcast_add_fusion.3, s32[108]{0:T(128)S(1)} %get-tuple-element.24, pred[108]{0:T(512)(128)(4,1)S(1)} %fusion.85), kind=kOutput, calls=%fused_computation.71 | convolution fusion | flops 286794432 | bytes 3540348 | tf_op jit(solution)/shard_map/dot_general | solution.py:26
  27.3 0.0 copy-done.1
  27.3 0.0 copy-done.12
  28.0 0.0 copy-done.3
  28.0 1.0 copy.21
  29.1 0.0 collective-permute-done.5.low_ref
  29.1 0.0 collective-permute-done.6.high_ref
  29.1 0.6 copy-done.5
  29.7 0.0 copy-done.6
  29.7 5.1 %shard_map.95.base_ref = f32[512,128]{1,0:T(8,128)} custom-call(s32[4,512]{1,0:T(4,128)} %nbr_ref.3, f32[32,128]{1,0:T(8,128)} %copy-done.5, f32[32,128]{1,0:T(8,128)} %copy-done.6, f32[2,512,128]{2,1,0:T(8,128)} %bitcast.48, f32[4,512,128]{2,1,0:T(8,128)} %bitcast.45), custom_call_target="tpu_custom_call" | custom-call | tf_op jit(solution)/shard_map/pallas_call | solution.py:80
  34.8 0.0 all-to-all-done
  34.8 33.2 %all_gather.11 = f32[512,128]{1,0:T(8,128)S(1)} all-gather(f32[64,128]{1,0:T(8,128)S(1)} %reduce_sum.9), channel_id=1, replica_groups=mesh['freq'=4,'mesh'=8] {'mesh'}, dimensions={0}, use_global_device_ids=true | all-gather | bytes 294912 | tf_op jit(solution)/shard_map/all_gather | solution.py:148
  68.0 0.9 slice.50
  68.9 0.8 slice.59
  69.8 2.1 %collective-permute-start.3 = (f32[40,4096]{1,0:T(8,128)}, f32[40,4096]{1,0:T(8,128)S(1)}, u32[]{:S(2)}, u32[]{:S(2)}) collective-permute-start(f32[40,4096]{1,0:T(8,128)} %slice.50), channel_id=1, source_target_pairs={{0,16},{8,24},{16,0},{24,8},{1,17},{9,25},{17,1},{25,9},{2,18},{10... | collective-permute-start | bytes 1966088 | tf_op jit(solution)/shard_map/ppermute | solution.py:112
  71.8 0.7 gather_fusion
  72.6 0.0 copy-start.10
  72.6 0.0 copy-start.11
  72.6 9.0 %fusion.16 = f32[128,2,128]{2,1,0:T(2,128)S(1)} fusion(f32[128,128,128]{2,1,0:T(8,128)} %param.10, f32[2,128,128]{2,1,0:T(8,128)S(1)} %bitcast.55, f32[128]{0:T(128)S(1)} %compare_convert_fusion), kind=kOutput, calls=%fused_computation.25 | convolution fusion | flops 25198592 | bytes 8651264 | tf_op jit(solution)/shard_map/rgp,gfp->rgf/dot_general | solution.py:165
  81.6 0.1 collective-permute-start.9
  81.7 0.7 fusion.83
  82.4 2.4 %collective-permute-start.7 = (f32[32,128]{1,0:T(8,128)S(1)}, f32[32,128]{1,0:T(8,128)S(1)}, u32[]{:S(2)}, u32[]{:S(2)}) collective-permute-start(f32[32,128]{1,0:T(8,128)S(1)} %get-tuple-element.17), channel_id=1, source_target_pairs={{0,1},{1,2},{2,3},{3,4},{4,5},{5,6},{6,7},{8,9},{9,10},{10,11},{11... | collective-permute-start | bytes 49160 | tf_op jit(solution)/shard_map/ppermute | solution.py:169
  84.9 0.6 select_multiply_fusion.1
  85.4 0.8 collective-permute-done.7.low_ref
  86.2 1.5 %collective-permute-start.8 = (f32[32,128]{1,0:T(8,128)S(1)}, f32[32,128]{1,0:T(8,128)S(1)}, u32[]{:S(2)}, u32[]{:S(2)}) collective-permute-start(f32[32,128]{1,0:T(8,128)S(1)} %get-tuple-element.16), channel_id=1, source_target_pairs={{1,0},{2,1},{3,2},{4,3},{5,4},{6,5},{7,6},{9,8},{10,9},{11,10},{12... | collective-permute-start | bytes 49160 | tf_op jit(solution)/shard_map/ppermute | solution.py:168
  87.7 1.0 slice.58
  88.7 3.4 %collective-permute-done.8.high_ref = f32[32,128]{1,0:T(8,128)S(1)} collective-permute-done((f32[32,128]{1,0:T(8,128)S(1)}, f32[32,128]{1,0:T(8,128)S(1)}, u32[]{:S(2)}, u32[]{:S(2)}) %collective-permute-start.8) | collective-permute-done | bytes 16416 | tf_op jit(solution)/shard_map/ppermute | solution.py:168
  92.2 0.0 copy-done.4
  92.2 0.6 copy-done.8
  92.7 5.4 %shard_map.96 = f32[2,512,128]{2,1,0:T(8,128)} custom-call(s32[4,512]{1,0:T(4,128)} %nbr_ref.3, f32[32,128]{1,0:T(8,128)} %copy-done.7, f32[32,128]{1,0:T(8,128)} %copy-done.8, f32[512,128]{1,0:T(8,128)} %shard_map.95.base_ref, f32[512,128]{1,0:T(8,128)} %bitcast.51, f32[2,128,128]{2,1,0:T(8,128)} %bitcast.54, f32[4,512,128]{2,1,0:T(8,128)} %bitcast.46), custom_call_target="tpu_custom_call" | custom-call | tf_op jit(solution)/shard_map/pallas_call | solution.py:80
  98.2 0.0 collective-permute-done.9
  98.2 0.0 collective-permute-start.10
  98.2 2.2 %reshape.192 = f32[1,2,65536]{2,1,0:T(2,128)} reshape(f32[2,512,128]{2,1,0:T(8,128)} %shard_map.96) | data formatting | bytes 1048576 | tf_op jit(solution)/shard_map/reshape | solution.py:176
  100.3 2.0 %fusion.35 = f32[108,4096]{1,0:T(8,128)S(1)} fusion(f32[28,4096]{1,0:T(8,128)} %collective-permute-done.9, f32[108,108]{1,0:T(8,128)S(1)} %get-tuple-element.18), kind=kOutput, calls=%fused_computation.48 | convolution fusion | flops 74317824 | bytes 2274880 | tf_op jit(solution)/shard_map/dot_general | solution.py:26
  102.3 0.0 collective-permute-done.1
  102.3 0.6 collective-permute-start.2
  102.9 0.0 collective-permute-done.3
  102.9 0.1 collective-permute-start.4
  103.0 0.9 fusion.38
  103.9 0.0 copy-start
  103.9 0.0 collective-permute-done.10
  103.9 2.1 %fusion.33 = f32[108,4096]{1,0:T(8,128)S(1)} fusion(f32[28,4096]{1,0:T(8,128)} %collective-permute-done.10, f32[108,108]{1,0:T(8,128)S(1)} %get-tuple-element.19), kind=kOutput, calls=%fused_computation.46 | convolution fusion | flops 74317824 | bytes 2274880 | tf_op jit(solution)/shard_map/dot_general | solution.py:26
  106.0 0.0 collective-permute-done
  106.1 2.8 %convolution_add_fusion.3 = f32[108,4096]{1,0:T(8,128)S(1)} fusion(f32[108,4096]{1,0:T(8,128)S(1)} %copy-done, f32[108,4096]{1,0:T(8,128)} %collective-permute-done, f32[108]{0:T(128)S(1)} %fusion.87, s32[108]{0:T(128)S(1)} %get-tuple-element.25, s32[108]{0:T(128)S(1)} %get-tuple-element.24, pred[108]{0:T(512)(128)(4,1)S(1)} %fusion.85), kind=kOutput, calls=%fused_computation.7 | convolution fusion | flops 287236800 | bytes 5309820 | tf_op jit(solution)/shard_map/dot_general | solution.py:26
  108.8 2.0 %convolution_add_fusion.2 = f32[108,4096]{1,0:T(8,128)S(1)} fusion(f32[108,4096]{1,0:T(8,128)S(1)} %convolution_add_fusion.3, f32[40,4096]{1,0:T(8,128)} %collective-permute-done.1, f32[108,108]{1,0:T(8,128)S(1)} %get-tuple-element.18), kind=kOutput, calls=%fused_computation.3 | convolution fusion | flops 106610688 | bytes 4240960 | tf_op jit(solution)/shard_map/dot_general | solution.py:26
  110.8 0.0 collective-permute-done.2
  110.8 1.0 fusion
  111.9 0.0 collective-permute-done.4
  111.9 2.5 %fusion.2 = f32[108,4096]{1,0:T(8,128)} fusion(f32[108,4096]{1,0:T(8,128)S(1)} %fusion.33, f32[108,4096]{1,0:T(8,128)S(1)} %fusion.35, f32[108,4096]{1,0:T(8,128)S(1)} %fusion, f32[40,4096]{1,0:T(8,128)S(1)} %collective-permute-done.4, f32[108,108]{1,0:T(8,128)S(1)} %get-tuple-element.19), kind=kOutput, calls=%fused_computation.6 | convolution fusion | flops 107495424 | bytes 7779904 | tf_op jit(solution)/shard_map/dot_general | solution.py:26
  (28 shorter events, 0.2 us)
Async XLA Ops:
  9.5 96.6 %collective-permute-start = (f32[108,4096]{1,0:T(8,128)S(1)}, f32[108,4096]{1,0:T(8,128)}, u32[]{:S(2)}, u32[]{:S(2)}) collective-permute-start(f32[108,4096]{1,0:T(8,128)S(1)} %reshape.186), channel_id=1, source_target_pairs={{0,8},{8,0},{16,24},{24,16},{1,9},{9,1},{17,25},{25,17},{2,10},{10... | collective-permute-start | bytes 5308424 | tf_op jit(solution)/shard_map/ppermute | solution.py:115
  10.8 8.2 %copy-start.2 = (f32[1,2,65536]{2,1,0:T(2,128)S(1)}, f32[1,2,65536]{2,1,0:T(2,128)}, u32[]{:S(2)}) copy-start(f32[1,2,65536]{2,1,0:T(2,128)} %param.13) | copy-start | bytes 1572868
  10.8 91.5 %collective-permute-start.1 = (f32[40,4096]{1,0:T(8,128)}, f32[40,4096]{1,0:T(8,128)}, u32[]{:S(2)}, u32[]{:S(2)}) collective-permute-start(f32[40,4096]{1,0:T(8,128)} %slice.47), channel_id=1, source_target_pairs={{0,16},{8,24},{16,0},{24,8},{1,17},{9,25},{17,1},{25,9},{2,18},{10... | collective-permute-start | bytes 1966088 | tf_op jit(solution)/shard_map/ppermute | solution.py:112
  15.6 19.2 %all-to-all-start = ((f32[4,64,128]{2,1,0:T(8,128)}), f32[4,64,128]{2,1,0:T(8,128)S(1)}, u32[]{:S(2)}, u32[]{:S(2)}) async-start(f32[4,64,128]{2,1,0:T(8,128)} %reshape.188), calls=%async_computation | async-start | bytes 262144 | tf_op jit(solution)/shard_map/all_to_all | solution.py:146
  19.0 8.4 %copy-start.1 = (f32[1,2,512,128]{3,2,1,0:T(8,128)}, f32[1,2,512,128]{3,2,1,0:T(8,128)S(1)}, u32[]{:S(2)}) copy-start(f32[1,2,512,128]{3,2,1,0:T(8,128)S(1)} %copy.22) | copy-start | bytes 1572868
  19.0 10.1 %collective-permute-start.5 = (f32[32,128]{1,0:T(8,128)S(1)}, f32[32,128]{1,0:T(8,128)S(1)}, u32[]{:S(2)}, u32[]{:S(2)}) collective-permute-start(f32[32,128]{1,0:T(8,128)S(1)} %get-tuple-element.15), channel_id=1, source_target_pairs={{0,1},{1,2},{2,3},{3,4},{4,5},{5,6},{6,7},{8,9},{9,10},{10,11},{11... | collective-permute-start | bytes 49160 | tf_op jit(solution)/shard_map/ppermute | solution.py:130
  22.4 6.7 %collective-permute-start.6 = (f32[32,128]{1,0:T(8,128)S(1)}, f32[32,128]{1,0:T(8,128)S(1)}, u32[]{:S(2)}, u32[]{:S(2)}) collective-permute-start(f32[32,128]{1,0:T(8,128)S(1)} %get-tuple-element.14), channel_id=1, source_target_pairs={{1,0},{2,1},{3,2},{4,3},{5,4},{6,5},{7,6},{9,8},{10,9},{11,10},{12... | collective-permute-start | bytes 49160 | tf_op jit(solution)/shard_map/ppermute | solution.py:131
  24.9 2.4 %copy-start.12 = (s32[128]{0:T(128)S(1)}, s32[128]{0:T(128)}, u32[]{:S(2)}) copy-start(s32[128]{0:T(128)} %param.11) | copy-start | bytes 1540
  24.9 3.1 %copy-start.3 = (f32[4,65536]{1,0:T(4,128)S(1)}, f32[4,65536]{1,0:T(4,128)}, u32[]{:S(2)}) copy-start(f32[4,65536]{1,0:T(4,128)} %param.15) | copy-start | bytes 3145732
  29.1 0.6 copy-start.5
  29.1 0.6 copy-start.6
  69.8 33.1 %collective-permute-start.3 = (f32[40,4096]{1,0:T(8,128)}, f32[40,4096]{1,0:T(8,128)S(1)}, u32[]{:S(2)}, u32[]{:S(2)}) collective-permute-start(f32[40,4096]{1,0:T(8,128)} %slice.50), channel_id=1, source_target_pairs={{0,16},{8,24},{16,0},{24,8},{1,17},{9,25},{17,1},{25,9},{2,18},{10... | collective-permute-start | bytes 1966088 | tf_op jit(solution)/shard_map/ppermute | solution.py:112
  72.5 12.3 %copy-start.9 = (f32[108]{0:T(128)S(1)}, f32[108]{0:T(128)}, u32[]{:S(2)}) copy-start(f32[108]{0:T(128)} %get-tuple-element.21) | copy-start | bytes 1300
  72.6 12.3 %copy-start.10 = (s32[108]{0:T(128)S(1)}, s32[108]{0:T(128)}, u32[]{:S(2)}) copy-start(s32[108]{0:T(128)} %get-tuple-element.22) | copy-start | bytes 1300
  72.6 12.3 %copy-start.11 = (s32[108]{0:T(128)S(1)}, s32[108]{0:T(128)}, u32[]{:S(2)}) copy-start(s32[108]{0:T(128)} %get-tuple-element.23) | copy-start | bytes 1300
  81.6 10.6 %copy-start.4 = (f32[128,2,128]{2,0,1:T(8,128)}, f32[128,2,128]{2,0,1:T(8,128)S(1)}, u32[]{:S(2)}) copy-start(f32[128,2,128]{2,0,1:T(8,128)S(1)} %copy.23) | copy-start | bytes 393220
  81.6 16.6 %collective-permute-start.9 = (f32[28,4096]{1,0:T(8,128)}, f32[28,4096]{1,0:T(8,128)}, u32[]{:S(2)}, u32[]{:S(2)}) collective-permute-start(f32[28,4096]{1,0:T(8,128)} %slice.59), channel_id=1, source_target_pairs={{0,16},{8,24},{16,0},{24,8},{1,17},{9,25},{17,1},{25,9},{2,18},{10... | collective-permute-start | bytes 1376264 | tf_op jit(solution)/shard_map/ppermute | solution.py:112
  82.4 3.8 %collective-permute-start.7 = (f32[32,128]{1,0:T(8,128)S(1)}, f32[32,128]{1,0:T(8,128)S(1)}, u32[]{:S(2)}, u32[]{:S(2)}) collective-permute-start(f32[32,128]{1,0:T(8,128)S(1)} %get-tuple-element.17), channel_id=1, source_target_pairs={{0,1},{1,2},{2,3},{3,4},{4,5},{5,6},{6,7},{8,9},{9,10},{10,11},{11... | collective-permute-start | bytes 49160 | tf_op jit(solution)/shard_map/ppermute | solution.py:169
  86.2 5.9 %copy-start.7 = (f32[32,128]{1,0:T(8,128)}, f32[32,128]{1,0:T(8,128)S(1)}, u32[]{:S(2)}) copy-start(f32[32,128]{1,0:T(8,128)S(1)} %collective-permute-done.7.low_ref) | copy-start | bytes 49156
  86.2 5.9 %collective-permute-start.8 = (f32[32,128]{1,0:T(8,128)S(1)}, f32[32,128]{1,0:T(8,128)S(1)}, u32[]{:S(2)}, u32[]{:S(2)}) collective-permute-start(f32[32,128]{1,0:T(8,128)S(1)} %get-tuple-element.16), channel_id=1, source_target_pairs={{1,0},{2,1},{3,2},{4,3},{5,4},{6,5},{7,6},{9,8},{10,9},{11,10},{12... | collective-permute-start | bytes 49160 | tf_op jit(solution)/shard_map/ppermute | solution.py:168
  92.2 0.6 copy-start.8
  98.2 5.8 %collective-permute-start.10 = (f32[28,4096]{1,0:T(8,128)}, f32[28,4096]{1,0:T(8,128)}, u32[]{:S(2)}, u32[]{:S(2)}) collective-permute-start(f32[28,4096]{1,0:T(8,128)} %collective-permute-done.9), channel_id=1, source_target_pairs={{0,8},{8,0},{16,24},{24,16},{1,9},{9,1},{17,25},{25,17},{2,10},{10... | collective-permute-start | bytes 1376264 | tf_op jit(solution)/shard_map/ppermute | solution.py:115
  102.3 8.5 %collective-permute-start.2 = (f32[40,4096]{1,0:T(8,128)}, f32[40,4096]{1,0:T(8,128)S(1)}, u32[]{:S(2)}, u32[]{:S(2)}) collective-permute-start(f32[40,4096]{1,0:T(8,128)} %collective-permute-done.1), channel_id=1, source_target_pairs={{0,8},{8,0},{16,24},{24,16},{1,9},{9,1},{17,25},{25,17},{2,10},{10... | collective-permute-start | bytes 1966088 | tf_op jit(solution)/shard_map/ppermute | solution.py:115
  102.9 9.0 %collective-permute-start.4 = (f32[40,4096]{1,0:T(8,128)S(1)}, f32[40,4096]{1,0:T(8,128)S(1)}, u32[]{:S(2)}, u32[]{:S(2)}) collective-permute-start(f32[40,4096]{1,0:T(8,128)S(1)} %collective-permute-done.3), channel_id=1, source_target_pairs={{0,8},{8,0},{16,24},{24,16},{1,9},{9,1},{17,25},{25,17},{2,10},{10... | collective-permute-start | bytes 1966088 | tf_op jit(solution)/shard_map/ppermute | solution.py:115
  103.9 2.1 %copy-start = (f32[108,4096]{1,0:T(8,128)S(1)}, f32[108,4096]{1,0:T(8,128)}, u32[]{:S(2)}) copy-start(f32[108,4096]{1,0:T(8,128)} %fusion.54) | copy-start | bytes 5308420
where the time goes:
time: 116 us; the launch traced here: 114 us
  blocking collectives  39.6 us (34%)
  matrix products  26.8 us (23%)
  starting transfers between devices  17 us (15%)
  local copies, waits for them, and re-layouts  12 us (10%)
  Pallas kernels  10.5 us (9%)
  waiting for transfers between devices  4.27 us (4%)
  other arithmetic  2.57 us (2%)
  between operations  1.65 us (1%)
    all_gather x1, blocking collectives, body(): table = lax.all_gather(weighted, 'mesh', axis=0, tiled=True)  33.2 us
    dot_general x9, matrix products, mm(): return jnp.dot(a, b, precision=high, preferred_element_type=jnp.float32)  16.2 us
    pallas_call x2, Pallas kernels, call(): pl.pallas_call(kernel, out_shape=jax.ShapeDtypeStruct(out_shape, jnp.floa...  10.5 us
    dot_general x1, matrix products, body(): push = jnp.einsum('rgp,gfp->rgf', picked, interp_weights, precision=high)  8.99 us
    all_gather x1, blocking collectives, body(): weights = lax.all_gather(time_weights, 'freq', axis=0)  6.32 us
    ppermute x3, starting transfers between devices, across(): lax.ppermute(x, 'freq', [(i, (i + d * cores) % nf) for i in range(nf)])  4.09 us
    ppermute x1, waiting for transfers between devices, body(): high1 = lax.ppermute(edge, 'mesh', down)  3.42 us
    ppermute x1, starting transfers between devices, body(): low0 = lax.ppermute(state[1, rows - halo:], 'mesh', up)  3.4 us
  transfers between devices with their start and end apart: 12, of which 2 were waited for; matrix products, arithmetic and copies ran while one was open for 31% of the time, Pallas kernels for 9%

commit v1 on v0

--- a/solution.py
+++ b/solution.py
@@ -116,8 +116,8 @@
 
     width = parts * local_freqs
     stacked = jnp.transpose(spectrum, (1, 0, 2)).reshape(width, points)
-    step = max(8, -(-3 * width // 8) // 8 * 8)
-    cuts = [(at, min(at + step, width)) for at in range(0, width, step)]
+    step = max(8, -(-7 * width // 16) // 8 * 8)
+    cuts = [(0, step), (step, width)]
 
     groups, block = interp_weights.shape[:2]
     faces, rows = neighbors.shape
@@ -145,16 +145,18 @@
     weighted = jnp.sum(
         lax.all_to_all(partial, "freq", split_axis=0, concat_axis=0, tiled=True), axis=0
     )
-    table = lax.all_gather(weighted, "mesh", axis=0, tiled=True)
-    table, stacked_late = lax.optimization_barrier((table, stacked))
-    tails = [
-        [across(stacked_late[slice(*cut)], d) for d in range(1, chips)] for cut in cuts[1:]
-    ]
+    table = lax.all_to_all(
+        jnp.broadcast_to(weighted, (nm, *weighted.shape)),
+        "mesh", split_axis=0, concat_axis=0, tiled=True,
+    ).reshape(nm * weighted.shape[0], block)
 
     base = call(
         first_kernel, (rows, lanes), rows, lanes, halo, faces,
         (neighbors, low0, high0, state, coup),
     )
+
+    head, stacked_late, base = lax.optimization_barrier((head, stacked, base))
+    tails = [[across(stacked_late[slice(*cuts[1])], d) for d in range(1, chips)]]
 
     owner = group_block // per_owner
     index = owner * (2 * per_owner) + group_block % per_owner

time: 116 us -> 89 us (0.77)
  the two profiles are of different devices: /device:TPU:0 before, /device:TPU:25 now
where the time goes in v1:
time: 89 us; the launch traced here: 88.2 us
  starting transfers between devices  25.5 us (29%)
  matrix products  25.2 us (28%)
  local copies, waits for them, and re-layouts  13.6 us (15%)
  Pallas kernels  10.5 us (12%)
  blocking collectives  6.35 us (7%)
  waiting for transfers between devices  4.09 us (5%)
  between operations  1.56 us (2%)
  other arithmetic  1.45 us (2%)
    dot_general x7, matrix products, mm(): return jnp.dot(a, b, precision=high, preferred_element_type=jnp.float32)  14.6 us
    pallas_call x2, Pallas kernels, call(): pl.pallas_call(kernel, out_shape=jax.ShapeDtypeStruct(out_shape, jnp.floa...  10.5 us
    dot_general x1, matrix products, body(): push = jnp.einsum('rgp,gfp->rgf', picked, interp_weights, precision=high)  9.04 us
    all_gather x1, blocking collectives, body(): weights = lax.all_gather(time_weights, 'freq', axis=0)  6.35 us
    all_to_all x1, starting transfers between devices, body(): lax.all_to_all(jnp.broadcast_to(weighted, (nm, *weighted.shape)), 'mesh',...  5.36 us
    unnamed x30, local copies, waits for them, and re-layouts  4.81 us
    ppermute x1, starting transfers between devices, body(): high1 = lax.ppermute(edge, 'mesh', down)  3.89 us
    all_to_all x1, starting transfers between devices, body(): lax.all_to_all(partial, 'freq', split_axis=0, concat_axis=0, tiled=True)  3.63 us
  transfers between devices with their start and end apart: 11, of which 3 were waited for; matrix products, arithmetic and copies ran while one was open for 36% of the time, Pallas kernels for 12%

profile of v1, /device:TPU:25, one launch (start us, length us, event | category | flops | bytes accessed | tf_op | source)
XLA Modules:
  0.0 88.2 jit_solution(7658251447619224370)
XLA Ops:
  0.6 1.1 %copy.22 = f32[1,2,512,128]{3,2,1,0:T(8,128)S(1)} copy(f32[1,2,512,128]{3,1,2,0:T(2,128)} %bitcast.50) | data formatting | bytes 1048576
  1.7 0.0 copy-start.2
  1.7 3.0 %collective-permute-start.3 = (f32[32,128]{1,0:T(8,128)S(1)}, f32[32,128]{1,0:T(8,128)S(1)}, u32[]{:S(2)}, u32[]{:S(2)}) collective-permute-start(f32[32,128]{1,0:T(8,128)S(1)} %get-tuple-element.16), channel_id=1, source_target_pairs={{1,0},{2,1},{3,2},{4,3},{5,4},{6,5},{7,6},{9,8},{10,9},{11,10},{12... | collective-permute-start | bytes 49160 | tf_op jit(solution)/shard_map/ppermute | solution.py:131
  4.7 2.3 %collective-permute-start.2 = (f32[32,128]{1,0:T(8,128)S(1)}, f32[32,128]{1,0:T(8,128)S(1)}, u32[]{:S(2)}, u32[]{:S(2)}) collective-permute-start(f32[32,128]{1,0:T(8,128)S(1)} %get-tuple-element.17), channel_id=1, source_target_pairs={{0,1},{1,2},{2,3},{3,4},{4,5},{5,6},{6,7},{8,9},{9,10},{10,11},{11... | collective-permute-start | bytes 49160 | tf_op jit(solution)/shard_map/ppermute | solution.py:130
  7.0 6.3 %all-gather.1 = f32[4,2,108]{2,1,0:T(2,128)S(1)} all-gather(f32[1,2,108]{2,1,0:T(2,128)} %bitcast.58), channel_id=2, replica_groups=mesh['freq'=4,'mesh'=8] {'freq'}, dimensions={0}, use_global_device_ids=true | all-gather | bytes 4320 | tf_op jit(solution)/shard_map/all_gather | solution.py:133
  13.4 2.5 %reshape.189 = f32[108,4096]{1,0:T(8,128)S(1)} reshape(f32[54,2,4096]{2,1,0:T(2,128)} %bitcast.49) | data formatting | bytes 3538944 | tf_op jit(solution)/shard_map/reshape | solution.py:118
  15.9 0.0 copy-done.2
  15.9 0.2 collective-permute-start
  16.2 1.6 %fusion.5 = f32[4,108,2]{1,2,0:T(2,128)S(1)} fusion(f32[4,2,108]{2,1,0:T(2,128)S(1)} %all-gather.1, f32[108]{0:T(128)S(1)} %fusion.84, s32[108]{0:T(128)S(1)} %broadcast_add_fusion.3, s32[4,108]{1,0:T(4,128)S(1)} %multiply_add_fusion, pred[108]{0:T(512)(128)(4,1)S(1)} %fusion.83), kind=kOutput, calls=%fused_computation.11 | convolution fusion | flops 1679616 | bytes 9612 | tf_op jit(solution)/shard_map/wsr,wrk->wsk/dot_general | solution.py:136
  17.7 0.6 fusion.98
  18.3 0.7 reshape.193
  19.0 3.6 %all-to-all-start = ((f32[4,64,128]{2,1,0:T(8,128)}), f32[4,64,128]{2,1,0:T(8,128)S(1)}, u32[]{:S(2)}, u32[]{:S(2)}) async-start(f32[4,64,128]{2,1,0:T(8,128)} %reshape.193), calls=%async_computation | async-start | bytes 262144 | tf_op jit(solution)/shard_map/all_to_all | solution.py:146
  22.6 0.9 %slice.38 = f32[48,4096]{1,0:T(8,128)} slice(f32[108,4096]{1,0:T(8,128)S(1)} %reshape.189), slice={[0:48], [0:4096]} | slice | bytes 1572864 | tf_op jit(solution)/shard_map/slice | solution.py:141
  23.5 1.4 %collective-permute-start.1 = (f32[48,4096]{1,0:T(8,128)}, f32[48,4096]{1,0:T(8,128)S(1)}, u32[]{:S(2)}, u32[]{:S(2)}) collective-permute-start(f32[48,4096]{1,0:T(8,128)} %slice.38), channel_id=1, source_target_pairs={{0,16},{8,24},{16,0},{24,8},{1,17},{9,25},{17,1},{25,9},{2,18},{10... | collective-permute-start | bytes 2359304 | tf_op jit(solution)/shard_map/ppermute | solution.py:112
  24.9 0.0 copy-done.13
  25.0 1.2 %all-to-all-done = f32[4,64,128]{2,1,0:T(8,128)S(1)} async-done(((f32[4,64,128]{2,1,0:T(8,128)}), f32[4,64,128]{2,1,0:T(8,128)S(1)}, u32[]{:S(2)}, u32[]{:S(2)}) %all-to-all-start) | async-done | bytes 131104 | tf_op jit(solution)/shard_map/all_to_all | solution.py:146
  26.2 0.7 broadcast_in_dim.57
  26.9 5.4 %all-to-all-start.1 = ((f32[8,64,128]{2,1,0:T(8,128)}), f32[8,64,128]{2,1,0:T(8,128)S(1)}, u32[]{:S(2)}, u32[]{:S(2)}) async-start(f32[8,64,128]{2,1,0:T(8,128)} %broadcast_in_dim.57), calls=%async_computation.1 | async-start | bytes 524288 | tf_op jit(solution)/shard_map/all_to_all | solution.py:148
  32.3 2.4 %fusion.52 = f32[108,4096]{1,0:T(8,128)} fusion(f32[108,4096]{1,0:T(8,128)S(1)} %reshape.189, f32[108]{0:T(128)S(1)} %fusion.84, s32[108]{0:T(128)S(1)} %broadcast_add_fusion.3, s32[108]{0:T(128)S(1)} %get-tuple-element.26, pred[108]{0:T(512)(128)(4,1)S(1)} %fusion.83), kind=kOutput, calls=%fused_computation.67 | convolution fusion | flops 286794432 | bytes 3540348 | tf_op jit(solution)/shard_map/dot_general | solution.py:26
  35.4 0.0 copy-done.5
  35.4 1.0 %copy.21 = f32[1,4,512,128]{3,2,1,0:T(8,128)} copy(f32[1,4,512,128]{3,1,2,0:T(4,128)S(1)} %bitcast.52) | data formatting | bytes 2097152
  36.4 0.0 collective-permute-done.3.high_ref
  36.4 0.0 collective-permute-done.2.low_ref
  36.4 0.0 copy-start.10
  36.4 0.6 copy-done.9
  37.0 0.0 copy-done.10
  37.0 5.1 %shard_map.95.base_ref = f32[512,128]{1,0:T(8,128)} custom-call(s32[4,512]{1,0:T(4,128)} %nbr_ref.3, f32[32,128]{1,0:T(8,128)} %copy-done.10, f32[32,128]{1,0:T(8,128)} %copy-done.9, f32[2,512,128]{2,1,0:T(8,128)} %bitcast.48, f32[4,512,128]{2,1,0:T(8,128)} %bitcast.44), custom_call_target="tpu_custom_call" | custom-call | tf_op jit(solution)/shard_map/pallas_call | solution.py:80
  42.1 1.2 %collective-permute-done.1 = f32[48,4096]{1,0:T(8,128)S(1)} collective-permute-done((f32[48,4096]{1,0:T(8,128)}, f32[48,4096]{1,0:T(8,128)S(1)}, u32[]{:S(2)}, u32[]{:S(2)}) %collective-permute-start.1) | collective-permute-done | bytes 786464 | tf_op jit(solution)/shard_map/ppermute | solution.py:112
  43.3 0.9 %copy-done.6 = f32[48,4096]{1,0:T(8,128)} copy-done((f32[48,4096]{1,0:T(8,128)}, f32[48,4096]{1,0:T(8,128)S(1)}, u32[]{:S(2)}) %copy-start.6) | copy-done | bytes 786456
  44.2 1.0 %slice.47 = f32[60,4096]{1,0:T(8,128)} slice(f32[108,4096]{1,0:T(8,128)S(1)} %reshape.189), slice={[48:108], [0:4096]} | slice | bytes 1966080 | tf_op jit(solution)/shard_map/slice | solution.py:159
  45.3 0.5 collective-permute-start.7
  45.8 0.0 all-to-all-done.1
  45.8 0.7 gather_fusion
  46.5 1.6 %collective-permute-start.4 = (f32[48,4096]{1,0:T(8,128)}, f32[48,4096]{1,0:T(8,128)}, u32[]{:S(2)}, u32[]{:S(2)}) collective-permute-start(f32[48,4096]{1,0:T(8,128)} %copy-done.6), channel_id=1, source_target_pairs={{0,8},{8,0},{16,24},{24,16},{1,9},{9,1},{17,25},{25,17},{2,10},{10... | collective-permute-start | bytes 2359304 | tf_op jit(solution)/shard_map/ppermute | solution.py:115
  48.1 9.0 %fusion.16 = f32[128,2,128]{2,1,0:T(2,128)S(1)} fusion(f32[128,128,128]{2,1,0:T(8,128)} %param.10, f32[2,128,128]{2,1,0:T(8,128)S(1)} %bitcast.55, f32[128]{0:T(128)S(1)} %compare_convert_fusion), kind=kOutput, calls=%fused_computation.23 | convolution fusion | flops 25198592 | bytes 8651264 | tf_op jit(solution)/shard_map/rgp,gfp->rgf/dot_general | solution.py:167
  57.2 0.0 copy-start.8
  57.2 0.8 fusion.81
  58.0 3.9 %collective-permute-start.6 = (f32[32,128]{1,0:T(8,128)S(1)}, f32[32,128]{1,0:T(8,128)S(1)}, u32[]{:S(2)}, u32[]{:S(2)}) collective-permute-start(f32[32,128]{1,0:T(8,128)S(1)} %get-tuple-element.18), channel_id=1, source_target_pairs={{1,0},{2,1},{3,2},{4,3},{5,4},{6,5},{7,6},{9,8},{10,9},{11,10},{12... | collective-permute-start | bytes 49160 | tf_op jit(solution)/shard_map/ppermute | solution.py:170
  61.9 2.1 %collective-permute-start.5 = (f32[32,128]{1,0:T(8,128)S(1)}, f32[32,128]{1,0:T(8,128)S(1)}, u32[]{:S(2)}, u32[]{:S(2)}) collective-permute-start(f32[32,128]{1,0:T(8,128)S(1)} %get-tuple-element.19), channel_id=1, source_target_pairs={{0,1},{1,2},{2,3},{3,4},{4,5},{5,6},{6,7},{8,9},{9,10},{10,11},{11... | collective-permute-start | bytes 49160 | tf_op jit(solution)/shard_map/ppermute | solution.py:171
  64.0 0.6 select_multiply_fusion.1
  64.5 0.0 copy-done.4
  64.6 1.0 %slice.46 = f32[1,1,65536]{2,1,0:T(1,128)} slice(f32[1,2,65536]{2,1,0:T(2,128)S(1)} %copy-done.4), slice={[0:1], [1:2], [0:65536]} | slice | bytes 524288 | tf_op jit(solution)/shard_map/slice | solution.py:174
  65.5 0.0 collective-permute-done.6.high_ref
  65.6 1.7 %collective-permute-done.5.low_ref = f32[32,128]{1,0:T(8,128)S(1)} collective-permute-done((f32[32,128]{1,0:T(8,128)S(1)}, f32[32,128]{1,0:T(8,128)S(1)}, u32[]{:S(2)}, u32[]{:S(2)}) %collective-permute-start.5) | collective-permute-done | bytes 16416 | tf_op jit(solution)/shard_map/ppermute | solution.py:171
  67.3 0.0 copy-done.8
  67.3 0.0 copy-done.11
  67.3 0.6 copy-done.12
  67.8 5.4 %shard_map.96 = f32[2,512,128]{2,1,0:T(8,128)} custom-call(s32[4,512]{1,0:T(4,128)} %nbr_ref.3, f32[32,128]{1,0:T(8,128)} %copy-done.12, f32[32,128]{1,0:T(8,128)} %copy-done.11, f32[512,128]{1,0:T(8,128)} %shard_map.95.base_ref, f32[512,128]{1,0:T(8,128)} %bitcast.51, f32[2,128,128]{2,1,0:T(8,128)} %bitcast.54, f32[4,512,128]{2,1,0:T(8,128)} %bitcast.45), custom_call_target="tpu_custom_call" | custom-call | tf_op jit(solution)/shard_map/pallas_call | solution.py:80
  73.3 0.0 collective-permute-done.7
  73.3 1.5 %collective-permute-start.8 = (f32[60,4096]{1,0:T(8,128)S(1)}, f32[60,4096]{1,0:T(8,128)}, u32[]{:S(2)}, u32[]{:S(2)}) collective-permute-start(f32[60,4096]{1,0:T(8,128)S(1)} %collective-permute-done.7), channel_id=1, source_target_pairs={{0,8},{8,0},{16,24},{24,16},{1,9},{9,1},{17,25},{25,17},{2,10},{10... | collective-permute-start | bytes 2949128 | tf_op jit(solution)/shard_map/ppermute | solution.py:115
  74.8 0.0 collective-permute-done.4
  74.8 3.2 %fusion.37 = f32[108,4096]{1,0:T(8,128)} fusion(f32[48,4096]{1,0:T(8,128)} %collective-permute-done.4, f32[108,108]{1,0:T(8,128)S(1)} %get-tuple-element.21), kind=kOutput, calls=%fused_computation.48 | convolution fusion | flops 127401984 | bytes 2602560 | tf_op jit(solution)/shard_map/dot_general | solution.py:26
  78.0 0.0 copy-done.3
  78.0 1.1 %reshape.196 = f32[1,2,65536]{2,1,0:T(2,128)} reshape(f32[2,512,128]{2,1,0:T(8,128)S(1)} %copy-done.3) | data formatting | bytes 1048576 | tf_op jit(solution)/shard_map/reshape | solution.py:178
  79.2 0.9 %fusion.35 = f32[108,4096]{1,0:T(8,128)S(1)} fusion(f32[60,4096]{1,0:T(8,128)S(1)} %collective-permute-done.7, f32[108,108]{1,0:T(8,128)S(1)} %get-tuple-element.20), kind=kOutput, calls=%fused_computation.46 | convolution fusion | flops 159252480 | bytes 2799168 | tf_op jit(solution)/shard_map/dot_general | solution.py:26
  80.1 0.0 collective-permute-done
  80.1 0.6 copy-done
  80.7 2.8 %convolution_add_fusion.1 = f32[108,4096]{1,0:T(8,128)S(1)} fusion(f32[108,4096]{1,0:T(8,128)S(1)} %copy-done, f32[108,4096]{1,0:T(8,128)} %collective-permute-done, f32[108]{0:T(128)S(1)} %fusion.85, s32[108]{0:T(128)S(1)} %get-tuple-element.27, s32[108]{0:T(128)S(1)} %get-tuple-element.26, pred[108]{0:T(512)(128)(4,1)S(1)} %fusion.83), kind=kOutput, calls=%fused_computation.5 | convolution fusion | flops 287236800 | bytes 5309820 | tf_op jit(solution)/shard_map/dot_general | solution.py:26
  83.4 0.0 copy-start.1
  83.4 0.0 copy-start.7
  83.4 0.0 collective-permute-done.8
  83.4 2.3 %fusion.33 = f32[108,4096]{1,0:T(8,128)S(1)} fusion(f32[60,4096]{1,0:T(8,128)} %collective-permute-done.8, f32[108,108]{1,0:T(8,128)S(1)} %get-tuple-element.21), kind=kOutput, calls=%fused_computation.44 | convolution fusion | flops 159252480 | bytes 2799168 | tf_op jit(solution)/shard_map/dot_general | solution.py:26
  85.8 0.0 copy-done.1
  85.8 2.5 %fusion.2 = f32[108,4096]{1,0:T(8,128)} fusion(f32[108,4096]{1,0:T(8,128)S(1)} %fusion.33, f32[108,4096]{1,0:T(8,128)S(1)} %fusion.35, f32[108,4096]{1,0:T(8,128)S(1)} %copy-done.1, f32[108,4096]{1,0:T(8,128)S(1)} %convolution_add_fusion.1, f32[48,4096]{1,0:T(8,128)S(1)} %copy-done.7, f32[108,108]{1,0:T(8,128)S(1)} %get-tuple-element.20), kind=kOutput, calls=%fused_computation.4 | convolution fusion | flops 129171456 | bytes 9680448 | tf_op jit(solution)/shard_map/dot_general | solution.py:26
  (25 shorter events, 0.1 us)
Async XLA Ops:
  1.7 14.2 %copy-start.2 = (f32[1,2,512,128]{3,2,1,0:T(8,128)}, f32[1,2,512,128]{3,2,1,0:T(8,128)S(1)}, u32[]{:S(2)}) copy-start(f32[1,2,512,128]{3,2,1,0:T(8,128)S(1)} %copy.22) | copy-start | bytes 1572868
  1.7 34.7 %collective-permute-start.3 = (f32[32,128]{1,0:T(8,128)S(1)}, f32[32,128]{1,0:T(8,128)S(1)}, u32[]{:S(2)}, u32[]{:S(2)}) collective-permute-start(f32[32,128]{1,0:T(8,128)S(1)} %get-tuple-element.16), channel_id=1, source_target_pairs={{1,0},{2,1},{3,2},{4,3},{5,4},{6,5},{7,6},{9,8},{10,9},{11,10},{12... | collective-permute-start | bytes 49160 | tf_op jit(solution)/shard_map/ppermute | solution.py:131
  4.7 31.7 %collective-permute-start.2 = (f32[32,128]{1,0:T(8,128)S(1)}, f32[32,128]{1,0:T(8,128)S(1)}, u32[]{:S(2)}, u32[]{:S(2)}) collective-permute-start(f32[32,128]{1,0:T(8,128)S(1)} %get-tuple-element.17), channel_id=1, source_target_pairs={{0,1},{1,2},{2,3},{3,4},{4,5},{5,6},{6,7},{8,9},{9,10},{10,11},{11... | collective-permute-start | bytes 49160 | tf_op jit(solution)/shard_map/ppermute | solution.py:130
  15.9 64.2 %collective-permute-start = (f32[108,4096]{1,0:T(8,128)S(1)}, f32[108,4096]{1,0:T(8,128)}, u32[]{:S(2)}, u32[]{:S(2)}) collective-permute-start(f32[108,4096]{1,0:T(8,128)S(1)} %reshape.189), channel_id=1, source_target_pairs={{0,8},{8,0},{16,24},{24,16},{1,9},{9,1},{17,25},{25,17},{2,10},{10... | collective-permute-start | bytes 5308424 | tf_op jit(solution)/shard_map/ppermute | solution.py:115
  17.7 7.2 %copy-start.13 = (s32[128]{0:T(128)S(1)}, s32[128]{0:T(128)}, u32[]{:S(2)}) copy-start(s32[128]{0:T(128)} %param.11) | copy-start | bytes 1540
  19.0 7.2 %all-to-all-start = ((f32[4,64,128]{2,1,0:T(8,128)}), f32[4,64,128]{2,1,0:T(8,128)S(1)}, u32[]{:S(2)}, u32[]{:S(2)}) async-start(f32[4,64,128]{2,1,0:T(8,128)} %reshape.193), calls=%async_computation | async-start | bytes 262144 | tf_op jit(solution)/shard_map/all_to_all | solution.py:146
  23.5 19.8 %collective-permute-start.1 = (f32[48,4096]{1,0:T(8,128)}, f32[48,4096]{1,0:T(8,128)S(1)}, u32[]{:S(2)}, u32[]{:S(2)}) collective-permute-start(f32[48,4096]{1,0:T(8,128)} %slice.38), channel_id=1, source_target_pairs={{0,16},{8,24},{16,0},{24,8},{1,17},{9,25},{17,1},{25,9},{2,18},{10... | collective-permute-start | bytes 2359304 | tf_op jit(solution)/shard_map/ppermute | solution.py:112
  26.9 18.8 %all-to-all-start.1 = ((f32[8,64,128]{2,1,0:T(8,128)}), f32[8,64,128]{2,1,0:T(8,128)S(1)}, u32[]{:S(2)}, u32[]{:S(2)}) async-start(f32[8,64,128]{2,1,0:T(8,128)} %broadcast_in_dim.57), calls=%async_computation.1 | async-start | bytes 524288 | tf_op jit(solution)/shard_map/all_to_all | solution.py:148
  32.3 3.1 %copy-start.5 = (f32[4,65536]{1,0:T(4,128)S(1)}, f32[4,65536]{1,0:T(4,128)}, u32[]{:S(2)}) copy-start(f32[4,65536]{1,0:T(4,128)} %param.15) | copy-start | bytes 3145732
  36.4 0.6 copy-start.9
  36.4 0.6 copy-start.10
  43.3 0.9 %copy-start.6 = (f32[48,4096]{1,0:T(8,128)}, f32[48,4096]{1,0:T(8,128)S(1)}, u32[]{:S(2)}) copy-start(f32[48,4096]{1,0:T(8,128)S(1)} %collective-permute-done.1) | copy-start | bytes 2359300
  45.3 28.0 %collective-permute-start.7 = (f32[60,4096]{1,0:T(8,128)}, f32[60,4096]{1,0:T(8,128)S(1)}, u32[]{:S(2)}, u32[]{:S(2)}) collective-permute-start(f32[60,4096]{1,0:T(8,128)} %slice.47), channel_id=1, source_target_pairs={{0,16},{8,24},{16,0},{24,8},{1,17},{9,25},{17,1},{25,9},{2,18},{10... | collective-permute-start | bytes 2949128 | tf_op jit(solution)/shard_map/ppermute | solution.py:112
  46.5 28.3 %collective-permute-start.4 = (f32[48,4096]{1,0:T(8,128)}, f32[48,4096]{1,0:T(8,128)}, u32[]{:S(2)}, u32[]{:S(2)}) collective-permute-start(f32[48,4096]{1,0:T(8,128)} %copy-done.6), channel_id=1, source_target_pairs={{0,8},{8,0},{16,24},{24,16},{1,9},{9,1},{17,25},{25,17},{2,10},{10... | collective-permute-start | bytes 2359304 | tf_op jit(solution)/shard_map/ppermute | solution.py:115
  48.1 16.5 %copy-start.4 = (f32[1,2,65536]{2,1,0:T(2,128)S(1)}, f32[1,2,65536]{2,1,0:T(2,128)}, u32[]{:S(2)}) copy-start(f32[1,2,65536]{2,1,0:T(2,128)} %param.13) | copy-start | bytes 1572868
  57.2 10.1 %copy-start.8 = (f32[128,2,128]{2,0,1:T(8,128)}, f32[128,2,128]{2,0,1:T(8,128)S(1)}, u32[]{:S(2)}) copy-start(f32[128,2,128]{2,0,1:T(8,128)S(1)} %copy.23) | copy-start | bytes 393220
  58.0 7.6 %collective-permute-start.6 = (f32[32,128]{1,0:T(8,128)S(1)}, f32[32,128]{1,0:T(8,128)S(1)}, u32[]{:S(2)}, u32[]{:S(2)}) collective-permute-start(f32[32,128]{1,0:T(8,128)S(1)} %get-tuple-element.18), channel_id=1, source_target_pairs={{1,0},{2,1},{3,2},{4,3},{5,4},{6,5},{7,6},{9,8},{10,9},{11,10},{12... | collective-permute-start | bytes 49160 | tf_op jit(solution)/shard_map/ppermute | solution.py:170
  61.9 5.4 %collective-permute-start.5 = (f32[32,128]{1,0:T(8,128)S(1)}, f32[32,128]{1,0:T(8,128)S(1)}, u32[]{:S(2)}, u32[]{:S(2)}) collective-permute-start(f32[32,128]{1,0:T(8,128)S(1)} %get-tuple-element.19), channel_id=1, source_target_pairs={{0,1},{1,2},{2,3},{3,4},{4,5},{5,6},{6,7},{8,9},{9,10},{10,11},{11... | collective-permute-start | bytes 49160 | tf_op jit(solution)/shard_map/ppermute | solution.py:171
  65.5 1.7 %copy-start.11 = (f32[32,128]{1,0:T(8,128)}, f32[32,128]{1,0:T(8,128)S(1)}, u32[]{:S(2)}) copy-start(f32[32,128]{1,0:T(8,128)S(1)} %collective-permute-done.6.high_ref) | copy-start | bytes 49156
  67.2 0.6 copy-start.12
  73.3 4.8 %copy-start.3 = (f32[2,512,128]{2,1,0:T(8,128)S(1)}, f32[2,512,128]{2,1,0:T(8,128)}, u32[]{:S(2)}) copy-start(f32[2,512,128]{2,1,0:T(8,128)} %shard_map.96) | copy-start | bytes 1572868
  73.3 10.2 %collective-permute-start.8 = (f32[60,4096]{1,0:T(8,128)S(1)}, f32[60,4096]{1,0:T(8,128)}, u32[]{:S(2)}, u32[]{:S(2)}) collective-permute-start(f32[60,4096]{1,0:T(8,128)S(1)} %collective-permute-done.7), channel_id=1, source_target_pairs={{0,8},{8,0},{16,24},{24,16},{1,9},{9,1},{17,25},{25,17},{2,10},{10... | collective-permute-start | bytes 2949128 | tf_op jit(solution)/shard_map/ppermute | solution.py:115
  79.2 1.5 %copy-start = (f32[108,4096]{1,0:T(8,128)S(1)}, f32[108,4096]{1,0:T(8,128)}, u32[]{:S(2)}) copy-start(f32[108,4096]{1,0:T(8,128)} %fusion.52) | copy-start | bytes 5308420
  83.4 2.3 %copy-start.1 = (f32[108,4096]{1,0:T(8,128)S(1)}, f32[108,4096]{1,0:T(8,128)}, u32[]{:S(2)}) copy-start(f32[108,4096]{1,0:T(8,128)} %fusion.37) | copy-start | bytes 5308420
  83.4 2.3 %copy-start.7 = (f32[48,4096]{1,0:T(8,128)S(1)}, f32[48,4096]{1,0:T(8,128)}, u32[]{:S(2)}) copy-start(f32[48,4096]{1,0:T(8,128)} %copy-done.6) | copy-start | bytes 2359300
